TPU v7x, 32 devices: a whole 2x2x4 slice. The times are simulated.
32 devices in a mesh: dp: 8 (over z, x), seq: 4 (over y, core).
Axes of the slice: x: 2, y: 2, z: 4, core: 2. Of those that a mesh axis runs over, the one named last changes fastest.
Arguments:
- queries: bfloat16 [4096, 2048], P(('dp', 'seq')), may hold values from -6 to 6
- keys: bfloat16 [4096, 2048], P(('dp', 'seq')), may hold values from -6 to 6
- values: bfloat16 [4096, 2048], P(('dp', 'seq')), may hold values from -6 to 6
- q_gain: float32 [2048], replicated, may hold values from 0.25 to 1.75
- k_gain: float32 [2048], replicated, may hold values from 0.25 to 1.75
- out_grad: bfloat16 [4096, 2048], P(('dp', 'seq')), may hold values from -16 to 16
- segments: int32 [8, 512], P('dp'), may hold values from 0 to 3, never falling along the last dimension, each value on 1 to 256 neighbouring positions
- visible: int32 [8, 512], P('dp'), may hold values 0 or 1
Outputs:
- attn_out: bfloat16 [4096, 2048], P(('dp', 'seq'))
- query_grad: bfloat16 [4096, 2048], P(('dp', 'seq'))
- key_grad: bfloat16 [4096, 2048], P(('dp', 'seq'))
- value_grad: bfloat16 [4096, 2048], P(('dp', 'seq'))
- q_gain_grad: float32 [2048], replicated
- k_gain_grad: float32 [2048], replicated
Inputs may be any that keep to these rules, and one draw needn't show every extreme that they name: `segments`: along each packed sequence the clip numbers never fall; each of the 4 clips holds 1 to 256 slots.
All inputs are finite; a program needn't handle non-finite values. No bound on the sum of `visible` on one device may be relied on, other than what follows from the above.
Results may differ from a plain program's by a relative error of at most 0.012.
The roundings to bfloat16 on the way count: a program that leaves them out, or rounds other values in their place, can miss the bound.
Values may be sent and summed in bfloat16 or wider, within the bound.
No kernel may reach another device: no remote copies, remote signals or barrier semaphores. Data moves between devices by JAX's collectives and lax.ppermute only.
A program may use at most 64 MiB of HBM per device.

v0:
```python
import jax
import jax.numpy as jnp
from jax import lax
from jax.sharding import PartitionSpec as P

D_HEAD = 128
epsilon = 1e-06


def normalize(raw_rows, gain_vec):
    raw_f32 = raw_rows.astype(jnp.float32)
    inv_rms = lax.rsqrt(jnp.mean(raw_f32 * raw_f32, axis=-1, keepdims=True) + epsilon)
    return ((raw_f32 * inv_rms * gain_vec).astype(jnp.bfloat16), inv_rms)


def norm_back(raw_rows, inv_rms, gain_vec, grad_norm):
    raw_f32 = raw_rows.astype(jnp.float32)
    grad_f32 = grad_norm.astype(jnp.float32)
    scaled_grad = gain_vec * grad_f32
    mean_term = jnp.mean(scaled_grad * raw_f32, axis=-1, keepdims=True)
    grad_raw = inv_rms * scaled_grad - raw_f32 * inv_rms**3 * mean_term
    return (grad_raw.astype(jnp.bfloat16), jnp.sum(grad_f32 * raw_f32 * inv_rms, axis=0))


def attend(q_norm, k_norm, val_rows, grad_rows, seg_row, vis_row, keep_out):
    seq_rows, feature_count = q_norm.shape
    head_count = feature_count // D_HEAD
    score_scale = D_HEAD ** (-0.5)
    block_rows = 512
    block_count = seq_rows // block_rows
    k_three = k_norm.reshape(seq_rows, head_count, D_HEAD)
    v_three = val_rows.reshape(seq_rows, head_count, D_HEAD)
    positions = jnp.arange(seq_rows, dtype=jnp.int32)
    key_open = vis_row == 1

    def one_block(totals, block_index):
        block_start = block_index * block_rows
        q_block = lax.dynamic_slice_in_dim(q_norm, block_start, block_rows, 0).reshape(
            block_rows, head_count, D_HEAD
        )
        seg_block = lax.dynamic_slice_in_dim(seg_row, block_start, block_rows, 0)
        pos_block = block_start + jnp.arange(block_rows, dtype=jnp.int32)
        allowed = (seg_block[:, None] == seg_row[None, :]) & (
            key_open[None, :] | (pos_block[:, None] == positions[None, :])
        )
        scores = (
            jnp.einsum("shd,thd->hst", q_block, k_three, preferred_element_type=jnp.float32)
            * score_scale
        )
        scores = jnp.where(allowed[None], scores, -1e30)
        row_max = jnp.max(scores, axis=-1, keepdims=True)
        weights = jnp.exp(scores - row_max)
        attn_prob = weights / jnp.sum(weights, axis=-1, keepdims=True)
        prob_half = attn_prob.astype(jnp.bfloat16)
        block_out = jnp.zeros((block_rows, feature_count), jnp.bfloat16)
        if keep_out:
            block_out = (
                jnp.einsum("hst,thd->shd", prob_half, v_three, preferred_element_type=jnp.float32)
                .reshape(block_rows, feature_count)
                .astype(jnp.bfloat16)
            )
        if grad_rows is None:
            return (totals, (block_out, block_out))
        grad_block = lax.dynamic_slice_in_dim(grad_rows, block_start, block_rows, 0).reshape(
            block_rows, head_count, D_HEAD
        )
        dprob = jnp.einsum("shd,thd->hst", grad_block, v_three, preferred_element_type=jnp.float32)
        value_add = jnp.einsum(
            "hst,shd->thd", prob_half, grad_block, preferred_element_type=jnp.float32
        )
        row_dot = jnp.sum(attn_prob * dprob, axis=-1, keepdims=True)
        score_grad = (attn_prob * (dprob - row_dot) * score_scale).astype(jnp.bfloat16)
        q_grad = (
            jnp.einsum("hst,thd->shd", score_grad, k_three, preferred_element_type=jnp.float32)
            .reshape(block_rows, feature_count)
            .astype(jnp.bfloat16)
        )
        key_add = jnp.einsum(
            "hst,shd->thd", score_grad, q_block, preferred_element_type=jnp.float32
        )
        return ((totals[0] + key_add, totals[1] + value_add), (block_out, q_grad))

    empty = jnp.zeros((seq_rows, head_count, D_HEAD), jnp.float32)
    totals, stacked = lax.scan(one_block, (empty, empty), jnp.arange(block_count, dtype=jnp.int32))
    attn_out = stacked[0].reshape(seq_rows, feature_count)
    if grad_rows is None:
        return attn_out
    q_grad = stacked[1].reshape(seq_rows, feature_count)
    k_grad = totals[0].reshape(seq_rows, feature_count).astype(jnp.bfloat16)
    v_grad = totals[1].reshape(seq_rows, feature_count).astype(jnp.bfloat16)
    return (attn_out, q_grad, k_grad, v_grad)


def per_device(queries, keys, values, q_gain, k_gain, out_grad, segments, visible):
    q_norm, q_inv = normalize(queries, q_gain)
    k_norm, k_inv = normalize(keys, k_gain)
    seg_row = segments[0]
    vis_row = visible[0]
    query_heads, key_heads, value_heads = (
        lax.all_to_all(q_norm, "seq", split_axis=1, concat_axis=0, tiled=True),
        lax.all_to_all(k_norm, "seq", split_axis=1, concat_axis=0, tiled=True),
        lax.all_to_all(values, "seq", split_axis=1, concat_axis=0, tiled=True),
    )
    out_part = attend(query_heads, key_heads, value_heads, None, seg_row, vis_row, True)
    attn_out = lax.all_to_all(out_part, "seq", split_axis=0, concat_axis=1, tiled=True)
    grad_heads = lax.all_to_all(out_grad, "seq", split_axis=1, concat_axis=0, tiled=True)
    unused_out, q_part, k_part, v_part = attend(
        query_heads, key_heads, value_heads, grad_heads, seg_row, vis_row, False
    )
    q_grad, k_grad, value_grad = (
        lax.all_to_all(q_part, "seq", split_axis=0, concat_axis=1, tiled=True),
        lax.all_to_all(k_part, "seq", split_axis=0, concat_axis=1, tiled=True),
        lax.all_to_all(v_part, "seq", split_axis=0, concat_axis=1, tiled=True),
    )
    query_grad, q_gain_part = norm_back(queries, q_inv, q_gain, q_grad)
    key_grad, k_gain_part = norm_back(keys, k_inv, k_gain, k_grad)
    q_gain_grad, k_gain_grad = lax.psum((q_gain_part, k_gain_part), ("dp", "seq"))
    return (attn_out, query_grad, key_grad, value_grad, q_gain_grad, k_gain_grad)


def solution(mesh):
    return jax.shard_map(
        per_device,
        mesh=mesh,
        in_specs=(
            P(("dp", "seq"), None),
            P(("dp", "seq"), None),
            P(("dp", "seq"), None),
            P(),
            P(),
            P(("dp", "seq"), None),
            P("dp", None),
            P("dp", None),
        ),
        out_specs=(
            P(("dp", "seq"), None),
            P(("dp", "seq"), None),
            P(("dp", "seq"), None),
            P(("dp", "seq"), None),
            P(),
            P(),
        ),
        check_vma=False,
    )
```

profile of v0, /device:TPU:0, one launch (start us, length us, event | category | flops | bytes accessed | tf_op | source)
XLA Modules:
  0.0 164.4 jit_solution(12461290162924541765)
XLA Ops:
  0.6 0.0 copy-start.1
  0.6 0.0 copy-start.5
  0.7 0.0 copy-start.2
  0.7 1.3 fusion.31
  2.0 1.2 fusion.33
  3.2 0.0 copy-start.3
  3.2 0.8 copy.112
  4.1 4.3 %all-to-all-start = ((bf16[128,4,512]{2,0,1:T(8,128)(2,1)}), bf16[128,4,512]{2,0,1:T(8,128)(2,1)S(1)}, u32[]{:S(2)}, u32[]{:S(2)}) async-start(bf16[128,4,512]{2,0,1:T(8,128)(2,1)} %bitcast.48), calls=%async_computation | async-start | bytes 1048576 | tf_op jit(solution)/shard_map/all_to_all | solution.py:100
  8.4 1.3 fusion.40
  9.6 0.0 copy-done.5
  9.6 0.2 fusion.42
  9.8 0.8 copy.111
  10.7 6.5 %all-to-all-done = bf16[128,4,512]{2,0,1:T(8,128)(2,1)S(1)} async-done(((bf16[128,4,512]{2,0,1:T(8,128)(2,1)}), bf16[128,4,512]{2,0,1:T(8,128)(2,1)S(1)}, u32[]{:S(2)}, u32[]{:S(2)}) %all-to-all-start) | async-done | bytes 524320 | tf_op jit(solution)/shard_map/all_to_all | solution.py:100
  17.2 3.5 %all-to-all-start.1 = ((bf16[128,4,512]{2,0,1:T(8,128)(2,1)}), bf16[128,4,512]{2,0,1:T(8,128)(2,1)S(1)}, u32[]{:S(2)}, u32[]{:S(2)}) async-start(bf16[128,4,512]{2,0,1:T(8,128)(2,1)} %bitcast.47), calls=%async_computation.1 | async-start | bytes 1048576 | tf_op jit(solution)/shard_map/all_to_all | solution.py:101
  20.7 0.8 copy.110
  21.5 7.9 %all-to-all-done.1 = bf16[128,4,512]{2,0,1:T(8,128)(2,1)S(1)} async-done(((bf16[128,4,512]{2,0,1:T(8,128)(2,1)}), bf16[128,4,512]{2,0,1:T(8,128)(2,1)S(1)}, u32[]{:S(2)}, u32[]{:S(2)}) %all-to-all-start.1) | async-done | bytes 524320 | tf_op jit(solution)/shard_map/all_to_all | solution.py:101
  29.4 3.5 %all-to-all-start.2 = ((bf16[128,4,512]{2,0,1:T(8,128)(2,1)}), bf16[128,4,512]{2,0,1:T(8,128)(2,1)S(1)}, u32[]{:S(2)}, u32[]{:S(2)}) async-start(bf16[128,4,512]{2,0,1:T(8,128)(2,1)} %bitcast.46), calls=%async_computation.2 | async-start | bytes 1048576 | tf_op jit(solution)/shard_map/all_to_all | solution.py:102
  32.9 0.8 copy.109
  33.8 7.9 %all-to-all-done.2 = bf16[128,4,512]{2,0,1:T(8,128)(2,1)S(1)} async-done(((bf16[128,4,512]{2,0,1:T(8,128)(2,1)}), bf16[128,4,512]{2,0,1:T(8,128)(2,1)S(1)}, u32[]{:S(2)}, u32[]{:S(2)}) %all-to-all-start.2) | async-done | bytes 524320 | tf_op jit(solution)/shard_map/all_to_all | solution.py:102
  41.7 3.5 %all-to-all-start.4 = ((bf16[128,4,512]{2,0,1:T(8,128)(2,1)}), bf16[128,4,512]{2,0,1:T(8,128)(2,1)S(1)}, u32[]{:S(2)}, u32[]{:S(2)}) async-start(bf16[128,4,512]{2,0,1:T(8,128)(2,1)} %bitcast.45), calls=%async_computation.4 | async-start | bytes 1048576 | tf_op jit(solution)/shard_map/all_to_all | solution.py:106
  45.2 0.3 fusion.52
  45.5 0.1 reshape.189
  45.6 1.1 copy.79
  46.7 0.1 reshape.190
  46.9 0.3 copy.75
  47.2 0.1 reshape.191
  47.3 6.6 %all-to-all-done.4 = bf16[128,4,512]{2,0,1:T(8,128)(2,1)S(1)} async-done(((bf16[128,4,512]{2,0,1:T(8,128)(2,1)}), bf16[128,4,512]{2,0,1:T(8,128)(2,1)S(1)}, u32[]{:S(2)}, u32[]{:S(2)}) %all-to-all-start.4) | async-done | bytes 524320 | tf_op jit(solution)/shard_map/all_to_all | solution.py:106
  53.9 0.1 reshape.192
  54.1 4.7 %fusion.66 = (f32[4,512]{1,0:T(4,128)S(1)}, f32[4,512,512]{1,2,0:T(8,128)}) fusion(pred[512,512]{0,1:T(8,128)(4,1)S(1)} %fusion.52, bf16[512,4,128]{0,2,1:T(8,128)(2,1)} %copy.79, bf16[512,4,128]{0,2,1:T(8,128)(2,1)S(1)} %copy.75), kind=kOutput, calls=%fused_computation.80 | convolution fusion | flops 272630272 | bytes 5513216 | tf_op jit(solution)/shard_map/while/body/eval_jaxpr/sub | solution.py:52
  58.7 2.9 %fusion.30 = bf16[512,4,128]{2,0,1:T(8,128)(2,1)S(1)} fusion(bf16[512,4,128]{2,1,0:T(4,128)(2,1)S(1)} %reshape.192, f32[4,512,512]{1,2,0:T(8,128)} %get-tuple-element.92, f32[4,512]{1,0:T(4,128)S(1)} %get-tuple-element.91), kind=kOutput, calls=%fused_computation.33 | convolution fusion | flops 270794752 | bytes 5251072 | tf_op jit(solution)/shard_map/while/body/eval_jaxpr/hst,shd->thd/dot_general | solution.py:68
  61.7 0.4 copy.84
  62.1 1.0 convert_element_type.117
  63.1 3.5 %all-to-all-start.7 = ((bf16[4,128,512]{2,1,0:T(8,128)(2,1)}), bf16[4,128,512]{2,1,0:T(8,128)(2,1)S(1)}, u32[]{:S(2)}, u32[]{:S(2)}) async-start(bf16[4,128,512]{2,1,0:T(8,128)(2,1)} %convert_element_type.117), calls=%async_computation.7 | async-start | bytes 1048576 | tf_op jit(solution)/shard_map/all_to_all | solution.py:113
  66.5 3.1 %fusion.29 = bf16[512,4,128]{2,0,1:T(8,128)(2,1)S(1)} fusion(bf16[512,4,128]{2,1,0:T(4,128)(2,1)S(1)} %reshape.191, f32[4,512,512]{1,2,0:T(8,128)} %get-tuple-element.92, f32[4,512]{1,0:T(4,128)S(1)} %get-tuple-element.91), kind=kOutput, calls=%fused_computation.32 | convolution fusion | flops 270794752 | bytes 5251072 | tf_op jit(solution)/shard_map/while/body/eval_jaxpr/hst,thd->shd/dot_general | solution.py:58
  69.6 0.4 copy.70
  70.1 1.0 convert_element_type.99
  71.1 4.3 %all-to-all-done.7 = bf16[4,128,512]{2,1,0:T(8,128)(2,1)S(1)} async-done(((bf16[4,128,512]{2,1,0:T(8,128)(2,1)}), bf16[4,128,512]{2,1,0:T(8,128)(2,1)S(1)}, u32[]{:S(2)}, u32[]{:S(2)}) %all-to-all-start.7) | async-done | bytes 524320 | tf_op jit(solution)/shard_map/all_to_all | solution.py:113
  75.3 3.5 %all-to-all-start.3 = ((bf16[4,128,512]{2,1,0:T(8,128)(2,1)}), bf16[4,128,512]{2,1,0:T(8,128)(2,1)S(1)}, u32[]{:S(2)}, u32[]{:S(2)}) async-start(bf16[4,128,512]{2,1,0:T(8,128)(2,1)} %convert_element_type.99), calls=%async_computation.3 | async-start | bytes 1048576 | tf_op jit(solution)/shard_map/all_to_all | solution.py:105
  78.8 2.7 %fusion.54 = f32[4,512,512]{1,2,0:T(8,128)} fusion(bf16[512,4,128]{2,1,0:T(4,128)(2,1)S(1)} %reshape.192, bf16[512,4,128]{2,1,0:T(4,128)(2,1)S(1)} %reshape.191), kind=kOutput, calls=%fused_computation.62 | convolution fusion | flops 268435456 | bytes 5242880 | tf_op jit(solution)/shard_map/while/body/eval_jaxpr/shd,thd->hst/dot_general | solution.py:67
  81.5 7.6 %fusion.23 = bf16[512,4,128]{0,2,1:T(8,128)(2,1)S(1)} fusion(bf16[512,4,128]{0,2,1:T(8,128)(2,1)} %copy.79, f32[4,512,512]{1,2,0:T(8,128)} %fusion.54, f32[4,512,512]{1,2,0:T(8,128)} %get-tuple-element.92, f32[4,512]{1,0:T(4,128)S(1)} %get-tuple-element.91), kind=kOutput, calls=%fused_computation.30 | convolution fusion | flops 276040192 | bytes 9445376 | tf_op jit(solution)/shard_map/while/body/eval_jaxpr/hst,shd->thd/dot_general | solution.py:78
  89.1 0.1 convert_element_type.110
  89.2 0.9 copy.81
  90.1 0.0 all-to-all-done.3
  90.1 3.5 %all-to-all-start.6 = ((bf16[4,128,512]{1,2,0:T(8,128)(2,1)}), bf16[4,128,512]{1,2,0:T(8,128)(2,1)S(1)}, u32[]{:S(2)}, u32[]{:S(2)}) async-start(bf16[4,128,512]{1,2,0:T(8,128)(2,1)} %copy.81), calls=%async_computation.6 | async-start | bytes 1048576 | tf_op jit(solution)/shard_map/all_to_all | solution.py:112
  93.6 8.5 %fusion.26 = bf16[512,4,128]{0,2,1:T(8,128)(2,1)} fusion(bf16[512,4,128]{0,2,1:T(8,128)(2,1)S(1)} %copy.75, f32[4,512,512]{1,2,0:T(8,128)} %fusion.54, f32[4,512,512]{1,2,0:T(8,128)} %get-tuple-element.92, f32[4,512]{1,0:T(4,128)S(1)} %get-tuple-element.91), kind=kOutput, calls=%fused_computation.31 | convolution fusion | flops 276040192 | bytes 9445376 | tf_op jit(solution)/shard_map/while/body/eval_jaxpr/hst,thd->shd/dot_general | solution.py:74
  102.1 1.2 convert_element_type.103
  103.3 0.9 copy.77
  104.2 0.0 all-to-all-done.6
  104.2 4.3 %all-to-all-start.5 = ((bf16[4,128,512]{1,2,0:T(8,128)(2,1)}), bf16[4,128,512]{1,2,0:T(8,128)(2,1)}, u32[]{:S(2)}, u32[]{:S(2)}) async-start(bf16[4,128,512]{1,2,0:T(8,128)(2,1)} %copy.77), calls=%async_computation.5 | async-start | bytes 1048576 | tf_op jit(solution)/shard_map/all_to_all | solution.py:111
  108.5 0.3 copy.85
  108.8 1.0 copy.89
  109.8 0.3 copy.71
  110.0 0.0 copy-start
  110.1 0.0 copy-start.4
  110.1 1.0 copy.88
  111.1 0.1 convert_element_type.121
  111.2 0.3 copy.82
  111.5 5.8 %all-to-all-done.5 = bf16[4,128,512]{1,2,0:T(8,128)(2,1)} async-done(((bf16[4,128,512]{1,2,0:T(8,128)(2,1)}), bf16[4,128,512]{1,2,0:T(8,128)(2,1)}, u32[]{:S(2)}, u32[]{:S(2)}) %all-to-all-start.5) | async-done | bytes 524320 | tf_op jit(solution)/shard_map/all_to_all | solution.py:111
  117.3 2.1 %convert_element_type.120 = f32[4,128,512]{1,2,0:T(8,128)} convert(bf16[4,128,512]{1,2,0:T(8,128)(2,1)} %all-to-all-done.5) | non-fusion elementwise | flops 262144 | bytes 1572864 | tf_op jit(solution)/shard_map/convert_element_type | solution.py:18
  119.4 1.6 copy.78
  121.0 0.6 fusion.39
  121.7 40.3 %all-reduce = (f32[2048]{0:T(1024)}, f32[2048]{0:T(1024)}) all-reduce(f32[2048]{0:T(1024)S(1)} %get-tuple-element.71, f32[2048]{0:T(1024)S(1)} %get-tuple-element.94), channel_id=1, replica_groups=mesh['dp'=8,'seq'=4] {'dp','seq'}, use_global_device_ids=true, to_apply=%region_8.9 | all-reduce | flops 4096 | bytes 32768 | tf_op jit(solution)/shard_map/psum | solution.py:117
  162.0 1.2 fusion.36
  163.2 1.2 fusion.45
  (14 shorter events, 0.1 us)
Async XLA Ops:
  0.6 9.0 %copy-start.1 = (bf16[128,2048]{1,0:T(8,128)(2,1)S(1)}, bf16[128,2048]{1,0:T(8,128)(2,1)}, u32[]{:S(2)}) copy-start(bf16[128,2048]{1,0:T(8,128)(2,1)} %param.9) | copy-start | bytes 1572868
  0.6 9.0 %copy-start.5 = (f32[2048]{0:T(1024)S(1)}, f32[2048]{0:T(1024)}, u32[]{:S(2)}) copy-start(f32[2048]{0:T(1024)} %param.12) | copy-start | bytes 24580
  0.7 20.0 %copy-start.2 = (bf16[128,2048]{1,0:T(8,128)(2,1)S(1)}, bf16[128,2048]{1,0:T(8,128)(2,1)}, u32[]{:S(2)}) copy-start(bf16[128,2048]{1,0:T(8,128)(2,1)} %param.10) | copy-start | bytes 1572868
  3.2 29.7 %copy-start.3 = (bf16[128,2048]{1,0:T(8,128)(2,1)S(1)}, bf16[128,2048]{1,0:T(8,128)(2,1)}, u32[]{:S(2)}) copy-start(bf16[128,2048]{1,0:T(8,128)(2,1)} %param.13) | copy-start | bytes 1572868
  4.1 13.1 %all-to-all-start = ((bf16[128,4,512]{2,0,1:T(8,128)(2,1)}), bf16[128,4,512]{2,0,1:T(8,128)(2,1)S(1)}, u32[]{:S(2)}, u32[]{:S(2)}) async-start(bf16[128,4,512]{2,0,1:T(8,128)(2,1)} %bitcast.48), calls=%async_computation | async-start | bytes 1048576 | tf_op jit(solution)/shard_map/all_to_all | solution.py:100
  8.3 36.8 %copy-start.7 = (s32[1,512]{1,0:T(1,128)S(1)}, s32[1,512]{1,0:T(1,128)}, u32[]{:S(2)}) copy-start(s32[1,512]{1,0:T(1,128)} %param.15) | copy-start | bytes 6148
  8.3 36.8 %copy-start.6 = (s32[1,512]{1,0:T(1,128)S(1)}, s32[1,512]{1,0:T(1,128)}, u32[]{:S(2)}) copy-start(s32[1,512]{1,0:T(1,128)} %param.14) | copy-start | bytes 6148
  17.2 12.3 %all-to-all-start.1 = ((bf16[128,4,512]{2,0,1:T(8,128)(2,1)}), bf16[128,4,512]{2,0,1:T(8,128)(2,1)S(1)}, u32[]{:S(2)}, u32[]{:S(2)}) async-start(bf16[128,4,512]{2,0,1:T(8,128)(2,1)} %bitcast.47), calls=%async_computation.1 | async-start | bytes 1048576 | tf_op jit(solution)/shard_map/all_to_all | solution.py:101
  29.4 12.3 %all-to-all-start.2 = ((bf16[128,4,512]{2,0,1:T(8,128)(2,1)}), bf16[128,4,512]{2,0,1:T(8,128)(2,1)S(1)}, u32[]{:S(2)}, u32[]{:S(2)}) async-start(bf16[128,4,512]{2,0,1:T(8,128)(2,1)} %bitcast.46), calls=%async_computation.2 | async-start | bytes 1048576 | tf_op jit(solution)/shard_map/all_to_all | solution.py:102
  41.7 12.3 %all-to-all-start.4 = ((bf16[128,4,512]{2,0,1:T(8,128)(2,1)}), bf16[128,4,512]{2,0,1:T(8,128)(2,1)S(1)}, u32[]{:S(2)}, u32[]{:S(2)}) async-start(bf16[128,4,512]{2,0,1:T(8,128)(2,1)} %bitcast.45), calls=%async_computation.4 | async-start | bytes 1048576 | tf_op jit(solution)/shard_map/all_to_all | solution.py:106
  63.1 12.3 %all-to-all-start.7 = ((bf16[4,128,512]{2,1,0:T(8,128)(2,1)}), bf16[4,128,512]{2,1,0:T(8,128)(2,1)S(1)}, u32[]{:S(2)}, u32[]{:S(2)}) async-start(bf16[4,128,512]{2,1,0:T(8,128)(2,1)} %convert_element_type.117), calls=%async_computation.7 | async-start | bytes 1048576 | tf_op jit(solution)/shard_map/all_to_all | solution.py:113
  75.3 14.8 %all-to-all-start.3 = ((bf16[4,128,512]{2,1,0:T(8,128)(2,1)}), bf16[4,128,512]{2,1,0:T(8,128)(2,1)S(1)}, u32[]{:S(2)}, u32[]{:S(2)}) async-start(bf16[4,128,512]{2,1,0:T(8,128)(2,1)} %convert_element_type.99), calls=%async_computation.3 | async-start | bytes 1048576 | tf_op jit(solution)/shard_map/all_to_all | solution.py:105
  90.1 14.0 %all-to-all-start.6 = ((bf16[4,128,512]{1,2,0:T(8,128)(2,1)}), bf16[4,128,512]{1,2,0:T(8,128)(2,1)S(1)}, u32[]{:S(2)}, u32[]{:S(2)}) async-start(bf16[4,128,512]{1,2,0:T(8,128)(2,1)} %copy.81), calls=%async_computation.6 | async-start | bytes 1048576 | tf_op jit(solution)/shard_map/all_to_all | solution.py:112
  104.2 13.2 %all-to-all-start.5 = ((bf16[4,128,512]{1,2,0:T(8,128)(2,1)}), bf16[4,128,512]{1,2,0:T(8,128)(2,1)}, u32[]{:S(2)}, u32[]{:S(2)}) async-start(bf16[4,128,512]{1,2,0:T(8,128)(2,1)} %copy.77), calls=%async_computation.5 | async-start | bytes 1048576 | tf_op jit(solution)/shard_map/all_to_all | solution.py:111
  110.0 10.9 %copy-start = (bf16[128,2048]{1,0:T(8,128)(2,1)S(1)}, bf16[128,2048]{1,0:T(8,128)(2,1)}, u32[]{:S(2)}) copy-start(bf16[128,2048]{1,0:T(8,128)(2,1)} %param.8) | copy-start | bytes 1572868
  110.1 10.9 %copy-start.4 = (f32[2048]{0:T(1024)S(1)}, f32[2048]{0:T(1024)}, u32[]{:S(2)}) copy-start(f32[2048]{0:T(1024)} %param.11) | copy-start | bytes 24580
where the time goes:
time: 165 us; the launch traced here: 164 us
  blocking collectives  40.3 us (24%)
  waiting for transfers between devices  39.1 us (24%)
  matrix products  29.5 us (18%)
  starting transfers between devices  29.4 us (18%)
  local copies, waits for them, and re-layouts  15.6 us (9%)
  other arithmetic  9.54 us (6%)
    psum x1, blocking collectives, per_device(): lax.psum((q_gain_part, k_gain_part), ('dp', 'seq'))  40.3 us
    dot_general x1, matrix products, one_block(): jnp.einsum('hst,thd->shd', score_grad, k_three, preferred_element_type=jn...  8.53 us
    all_to_all x1, waiting for transfers between devices, per_device(): lax.all_to_all(k_norm, 'seq', split_axis=1, concat_axis=0, tiled=True)  7.93 us
    all_to_all x1, waiting for transfers between devices, per_device(): lax.all_to_all(values, 'seq', split_axis=1, concat_axis=0, tiled=True)  7.93 us
    dot_general x1, matrix products, one_block(): jnp.einsum('hst,shd->thd', score_grad, q_block, preferred_element_type=jn...  7.62 us
    all_to_all x1, waiting for transfers between devices, per_device(): lax.all_to_all(out_grad, 'seq', split_axis=1, concat_axis=0, tiled=True)  6.63 us
    all_to_all x1, waiting for transfers between devices, per_device(): lax.all_to_all(q_norm, 'seq', split_axis=1, concat_axis=0, tiled=True)  6.49 us
    all_to_all x1, waiting for transfers between devices, per_device(): lax.all_to_all(q_part, 'seq', split_axis=0, concat_axis=1, tiled=True)  5.84 us
  transfers between devices with their start and end apart: 8, of which 6 were waited for; matrix products, arithmetic and copies ran while one was open for 22% of the time, Pallas kernels for 0%

commit v1 on v0

--- a/solution.py
+++ b/solution.py
@@ -114,7 +114,7 @@
     )
     query_grad, q_gain_part = norm_back(queries, q_inv, q_gain, q_grad)
     key_grad, k_gain_part = norm_back(keys, k_inv, k_gain, k_grad)
-    q_gain_grad, k_gain_grad = lax.psum((q_gain_part, k_gain_part), ("dp", "seq"))
+    q_gain_grad, k_gain_grad = lax.psum(lax.psum((q_gain_part, k_gain_part), "dp"), "seq")
     return (attn_out, query_grad, key_grad, value_grad, q_gain_grad, k_gain_grad)
 
 

time: 165 us -> 174 us (1.055)
  blocking collectives: 40.3 us -> 48.8 us
    psum x1 -> x2, blocking collectives: 40.3 us -> 48.8 us  [the longest x1 38 us: per_device(): lax.psum((q_gain_part, k_gain_part), 'dp')]
  transfers between devices with their start and end apart: 8 -> 8, of which waited for: 6 -> 6; matrix products, arithmetic and copies ran while one was open for 22% -> 20% of each run, Pallas kernels for 0% -> 0%
where the time goes in v1:
time: 174 us; the launch traced here: 173 us
  blocking collectives  48.8 us (28%)
  waiting for transfers between devices  39.1 us (22%)
  matrix products  29.5 us (17%)
  starting transfers between devices  29.4 us (17%)
  local copies, waits for them, and re-layouts  15.6 us (9%)
  other arithmetic  9.53 us (5%)
    psum x1, blocking collectives, per_device(): lax.psum((q_gain_part, k_gain_part), 'dp')  38 us
    psum x1, blocking collectives, per_device(): lax.psum(lax.psum((q_gain_part, k_gain_part), 'dp'), 'seq')  10.7 us
    dot_general x1, matrix products, one_block(): jnp.einsum('hst,thd->shd', score_grad, k_three, preferred_element_type=jn...  8.53 us
    all_to_all x1, waiting for transfers between devices, per_device(): lax.all_to_all(k_norm, 'seq', split_axis=1, concat_axis=0, tiled=True)  7.93 us
    all_to_all x1, waiting for transfers between devices, per_device(): lax.all_to_all(values, 'seq', split_axis=1, concat_axis=0, tiled=True)  7.93 us
    dot_general x1, matrix products, one_block(): jnp.einsum('hst,shd->thd', score_grad, q_block, preferred_element_type=jn...  7.62 us
    all_to_all x1, waiting for transfers between devices, per_device(): lax.all_to_all(out_grad, 'seq', split_axis=1, concat_axis=0, tiled=True)  6.63 us
    all_to_all x1, waiting for transfers between devices, per_device(): lax.all_to_all(q_norm, 'seq', split_axis=1, concat_axis=0, tiled=True)  6.49 us
  transfers between devices with their start and end apart: 8, of which 6 were waited for; matrix products, arithmetic and copies ran while one was open for 20% of the time, Pallas kernels for 0%

profile of v1, /device:TPU:0, one launch (start us, length us, event | category | flops | bytes accessed | tf_op | source)
XLA Modules:
  0.0 172.9 jit_solution(5972317618414314924)
XLA Ops:
  0.6 0.0 copy-start.1
  0.6 0.0 copy-start.5
  0.7 0.0 copy-start.2
  0.7 1.3 fusion.31
  2.0 1.2 fusion.33
  3.2 0.0 copy-start.3
  3.2 0.8 copy.112
  4.1 4.3 %all-to-all-start = ((bf16[128,4,512]{2,0,1:T(8,128)(2,1)}), bf16[128,4,512]{2,0,1:T(8,128)(2,1)S(1)}, u32[]{:S(2)}, u32[]{:S(2)}) async-start(bf16[128,4,512]{2,0,1:T(8,128)(2,1)} %bitcast.48), calls=%async_computation | async-start | bytes 1048576 | tf_op jit(solution)/shard_map/all_to_all | solution.py:100
  8.4 1.3 fusion.40
  9.6 0.2 fusion.42
  9.8 0.8 copy.111
  10.7 6.5 %all-to-all-done = bf16[128,4,512]{2,0,1:T(8,128)(2,1)S(1)} async-done(((bf16[128,4,512]{2,0,1:T(8,128)(2,1)}), bf16[128,4,512]{2,0,1:T(8,128)(2,1)S(1)}, u32[]{:S(2)}, u32[]{:S(2)}) %all-to-all-start) | async-done | bytes 524320 | tf_op jit(solution)/shard_map/all_to_all | solution.py:100
  17.2 3.5 %all-to-all-start.1 = ((bf16[128,4,512]{2,0,1:T(8,128)(2,1)}), bf16[128,4,512]{2,0,1:T(8,128)(2,1)S(1)}, u32[]{:S(2)}, u32[]{:S(2)}) async-start(bf16[128,4,512]{2,0,1:T(8,128)(2,1)} %bitcast.47), calls=%async_computation.1 | async-start | bytes 1048576 | tf_op jit(solution)/shard_map/all_to_all | solution.py:101
  20.7 0.8 copy.110
  21.5 7.9 %all-to-all-done.1 = bf16[128,4,512]{2,0,1:T(8,128)(2,1)S(1)} async-done(((bf16[128,4,512]{2,0,1:T(8,128)(2,1)}), bf16[128,4,512]{2,0,1:T(8,128)(2,1)S(1)}, u32[]{:S(2)}, u32[]{:S(2)}) %all-to-all-start.1) | async-done | bytes 524320 | tf_op jit(solution)/shard_map/all_to_all | solution.py:101
  29.4 3.5 %all-to-all-start.2 = ((bf16[128,4,512]{2,0,1:T(8,128)(2,1)}), bf16[128,4,512]{2,0,1:T(8,128)(2,1)S(1)}, u32[]{:S(2)}, u32[]{:S(2)}) async-start(bf16[128,4,512]{2,0,1:T(8,128)(2,1)} %bitcast.46), calls=%async_computation.2 | async-start | bytes 1048576 | tf_op jit(solution)/shard_map/all_to_all | solution.py:102
  32.9 0.8 copy.109
  33.8 7.9 %all-to-all-done.2 = bf16[128,4,512]{2,0,1:T(8,128)(2,1)S(1)} async-done(((bf16[128,4,512]{2,0,1:T(8,128)(2,1)}), bf16[128,4,512]{2,0,1:T(8,128)(2,1)S(1)}, u32[]{:S(2)}, u32[]{:S(2)}) %all-to-all-start.2) | async-done | bytes 524320 | tf_op jit(solution)/shard_map/all_to_all | solution.py:102
  41.7 3.5 %all-to-all-start.4 = ((bf16[128,4,512]{2,0,1:T(8,128)(2,1)}), bf16[128,4,512]{2,0,1:T(8,128)(2,1)S(1)}, u32[]{:S(2)}, u32[]{:S(2)}) async-start(bf16[128,4,512]{2,0,1:T(8,128)(2,1)} %bitcast.45), calls=%async_computation.4 | async-start | bytes 1048576 | tf_op jit(solution)/shard_map/all_to_all | solution.py:106
  45.2 0.3 fusion.52
  45.5 0.1 reshape.189
  45.6 1.1 copy.79
  46.7 0.1 reshape.190
  46.9 0.3 copy.75
  47.2 0.1 reshape.191
  47.3 6.6 %all-to-all-done.4 = bf16[128,4,512]{2,0,1:T(8,128)(2,1)S(1)} async-done(((bf16[128,4,512]{2,0,1:T(8,128)(2,1)}), bf16[128,4,512]{2,0,1:T(8,128)(2,1)S(1)}, u32[]{:S(2)}, u32[]{:S(2)}) %all-to-all-start.4) | async-done | bytes 524320 | tf_op jit(solution)/shard_map/all_to_all | solution.py:106
  53.9 0.1 reshape.192
  54.1 4.7 %fusion.66 = (f32[4,512]{1,0:T(4,128)S(1)}, f32[4,512,512]{1,2,0:T(8,128)}) fusion(pred[512,512]{0,1:T(8,128)(4,1)S(1)} %fusion.52, bf16[512,4,128]{0,2,1:T(8,128)(2,1)} %copy.79, bf16[512,4,128]{0,2,1:T(8,128)(2,1)S(1)} %copy.75), kind=kOutput, calls=%fused_computation.80 | convolution fusion | flops 272630272 | bytes 5513216 | tf_op jit(solution)/shard_map/while/body/eval_jaxpr/sub | solution.py:52
  58.7 2.9 %fusion.30 = bf16[512,4,128]{2,0,1:T(8,128)(2,1)S(1)} fusion(bf16[512,4,128]{2,1,0:T(4,128)(2,1)S(1)} %reshape.192, f32[4,512,512]{1,2,0:T(8,128)} %get-tuple-element.94, f32[4,512]{1,0:T(4,128)S(1)} %get-tuple-element.93), kind=kOutput, calls=%fused_computation.33 | convolution fusion | flops 270794752 | bytes 5251072 | tf_op jit(solution)/shard_map/while/body/eval_jaxpr/hst,shd->thd/dot_general | solution.py:68
  61.7 0.4 copy.84
  62.1 1.0 convert_element_type.117
  63.1 3.5 %all-to-all-start.7 = ((bf16[4,128,512]{2,1,0:T(8,128)(2,1)}), bf16[4,128,512]{2,1,0:T(8,128)(2,1)S(1)}, u32[]{:S(2)}, u32[]{:S(2)}) async-start(bf16[4,128,512]{2,1,0:T(8,128)(2,1)} %convert_element_type.117), calls=%async_computation.7 | async-start | bytes 1048576 | tf_op jit(solution)/shard_map/all_to_all | solution.py:113
  66.5 3.1 %fusion.29 = bf16[512,4,128]{2,0,1:T(8,128)(2,1)S(1)} fusion(bf16[512,4,128]{2,1,0:T(4,128)(2,1)S(1)} %reshape.191, f32[4,512,512]{1,2,0:T(8,128)} %get-tuple-element.94, f32[4,512]{1,0:T(4,128)S(1)} %get-tuple-element.93), kind=kOutput, calls=%fused_computation.32 | convolution fusion | flops 270794752 | bytes 5251072 | tf_op jit(solution)/shard_map/while/body/eval_jaxpr/hst,thd->shd/dot_general | solution.py:58
  69.6 0.4 copy.70
  70.1 1.0 convert_element_type.99
  71.1 4.3 %all-to-all-done.7 = bf16[4,128,512]{2,1,0:T(8,128)(2,1)S(1)} async-done(((bf16[4,128,512]{2,1,0:T(8,128)(2,1)}), bf16[4,128,512]{2,1,0:T(8,128)(2,1)S(1)}, u32[]{:S(2)}, u32[]{:S(2)}) %all-to-all-start.7) | async-done | bytes 524320 | tf_op jit(solution)/shard_map/all_to_all | solution.py:113
  75.3 3.5 %all-to-all-start.3 = ((bf16[4,128,512]{2,1,0:T(8,128)(2,1)}), bf16[4,128,512]{2,1,0:T(8,128)(2,1)S(1)}, u32[]{:S(2)}, u32[]{:S(2)}) async-start(bf16[4,128,512]{2,1,0:T(8,128)(2,1)} %convert_element_type.99), calls=%async_computation.3 | async-start | bytes 1048576 | tf_op jit(solution)/shard_map/all_to_all | solution.py:105
  78.8 2.7 %fusion.54 = f32[4,512,512]{1,2,0:T(8,128)} fusion(bf16[512,4,128]{2,1,0:T(4,128)(2,1)S(1)} %reshape.192, bf16[512,4,128]{2,1,0:T(4,128)(2,1)S(1)} %reshape.191), kind=kOutput, calls=%fused_computation.62 | convolution fusion | flops 268435456 | bytes 5242880 | tf_op jit(solution)/shard_map/while/body/eval_jaxpr/shd,thd->hst/dot_general | solution.py:67
  81.5 7.6 %fusion.23 = bf16[512,4,128]{0,2,1:T(8,128)(2,1)S(1)} fusion(bf16[512,4,128]{0,2,1:T(8,128)(2,1)} %copy.79, f32[4,512,512]{1,2,0:T(8,128)} %fusion.54, f32[4,512,512]{1,2,0:T(8,128)} %get-tuple-element.94, f32[4,512]{1,0:T(4,128)S(1)} %get-tuple-element.93), kind=kOutput, calls=%fused_computation.30 | convolution fusion | flops 276040192 | bytes 9445376 | tf_op jit(solution)/shard_map/while/body/eval_jaxpr/hst,shd->thd/dot_general | solution.py:78
  89.1 0.1 convert_element_type.110
  89.2 0.9 copy.81
  90.1 0.0 all-to-all-done.3
  90.1 3.5 %all-to-all-start.6 = ((bf16[4,128,512]{1,2,0:T(8,128)(2,1)}), bf16[4,128,512]{1,2,0:T(8,128)(2,1)S(1)}, u32[]{:S(2)}, u32[]{:S(2)}) async-start(bf16[4,128,512]{1,2,0:T(8,128)(2,1)} %copy.81), calls=%async_computation.6 | async-start | bytes 1048576 | tf_op jit(solution)/shard_map/all_to_all | solution.py:112
  93.6 8.5 %fusion.26 = bf16[512,4,128]{0,2,1:T(8,128)(2,1)} fusion(bf16[512,4,128]{0,2,1:T(8,128)(2,1)S(1)} %copy.75, f32[4,512,512]{1,2,0:T(8,128)} %fusion.54, f32[4,512,512]{1,2,0:T(8,128)} %get-tuple-element.94, f32[4,512]{1,0:T(4,128)S(1)} %get-tuple-element.93), kind=kOutput, calls=%fused_computation.31 | convolution fusion | flops 276040192 | bytes 9445376 | tf_op jit(solution)/shard_map/while/body/eval_jaxpr/hst,thd->shd/dot_general | solution.py:74
  102.1 1.2 convert_element_type.103
  103.3 0.9 copy.77
  104.2 0.0 all-to-all-done.6
  104.2 4.3 %all-to-all-start.5 = ((bf16[4,128,512]{1,2,0:T(8,128)(2,1)}), bf16[4,128,512]{1,2,0:T(8,128)(2,1)}, u32[]{:S(2)}, u32[]{:S(2)}) async-start(bf16[4,128,512]{1,2,0:T(8,128)(2,1)} %copy.77), calls=%async_computation.5 | async-start | bytes 1048576 | tf_op jit(solution)/shard_map/all_to_all | solution.py:111
  108.5 0.3 copy.85
  108.8 1.0 copy.89
  109.8 0.3 copy.71
  110.0 0.0 copy-start
  110.1 0.0 copy-start.4
  110.1 1.0 copy.88
  111.1 0.1 convert_element_type.121
  111.2 0.3 copy.82
  111.5 5.8 %all-to-all-done.5 = bf16[4,128,512]{1,2,0:T(8,128)(2,1)} async-done(((bf16[4,128,512]{1,2,0:T(8,128)(2,1)}), bf16[4,128,512]{1,2,0:T(8,128)(2,1)}, u32[]{:S(2)}, u32[]{:S(2)}) %all-to-all-start.5) | async-done | bytes 524320 | tf_op jit(solution)/shard_map/all_to_all | solution.py:111
  117.3 2.1 %convert_element_type.120 = f32[4,128,512]{1,2,0:T(8,128)} convert(bf16[4,128,512]{1,2,0:T(8,128)(2,1)} %all-to-all-done.5) | non-fusion elementwise | flops 262144 | bytes 1572864 | tf_op jit(solution)/shard_map/convert_element_type | solution.py:18
  119.4 1.6 copy.78
  121.0 0.6 fusion.39
  121.7 38.0 %all-reduce = (f32[2048]{0:T(1024)S(1)}, f32[2048]{0:T(1024)S(1)}) all-reduce(f32[2048]{0:T(1024)S(1)} %get-tuple-element.71, f32[2048]{0:T(1024)S(1)} %get-tuple-element.96), channel_id=1, replica_groups=mesh['dp'=8,'seq'=4] {'dp'}, use_global_device_ids=true, to_apply=%region_8.9 | all-reduce | flops 4096 | bytes 32768 | tf_op jit(solution)/shard_map/psum | solution.py:117
  159.7 10.7 %all-reduce.1 = (f32[2048]{0:T(1024)}, f32[2048]{0:T(1024)}) all-reduce(f32[2048]{0:T(1024)S(1)} %get-tuple-element.85, f32[2048]{0:T(1024)S(1)} %get-tuple-element.86), channel_id=1, replica_groups=mesh['dp'=8,'seq'=4] {'seq'}, use_global_device_ids=true, to_apply=%region_9.10 | all-reduce | flops 4096 | bytes 32768 | tf_op jit(solution)/shard_map/psum | solution.py:117
  170.4 1.2 fusion.36
  171.6 1.2 fusion.45
  (15 shorter events, 0.1 us)
Async XLA Ops:
  0.6 9.0 %copy-start.1 = (bf16[128,2048]{1,0:T(8,128)(2,1)S(1)}, bf16[128,2048]{1,0:T(8,128)(2,1)}, u32[]{:S(2)}) copy-start(bf16[128,2048]{1,0:T(8,128)(2,1)} %param.9) | copy-start | bytes 1572868
  0.6 9.0 %copy-start.5 = (f32[2048]{0:T(1024)S(1)}, f32[2048]{0:T(1024)}, u32[]{:S(2)}) copy-start(f32[2048]{0:T(1024)} %param.12) | copy-start | bytes 24580
  0.7 20.0 %copy-start.2 = (bf16[128,2048]{1,0:T(8,128)(2,1)S(1)}, bf16[128,2048]{1,0:T(8,128)(2,1)}, u32[]{:S(2)}) copy-start(bf16[128,2048]{1,0:T(8,128)(2,1)} %param.10) | copy-start | bytes 1572868
  3.2 29.7 %copy-start.3 = (bf16[128,2048]{1,0:T(8,128)(2,1)S(1)}, bf16[128,2048]{1,0:T(8,128)(2,1)}, u32[]{:S(2)}) copy-start(bf16[128,2048]{1,0:T(8,128)(2,1)} %param.13) | copy-start | bytes 1572868
  4.1 13.1 %all-to-all-start = ((bf16[128,4,512]{2,0,1:T(8,128)(2,1)}), bf16[128,4,512]{2,0,1:T(8,128)(2,1)S(1)}, u32[]{:S(2)}, u32[]{:S(2)}) async-start(bf16[128,4,512]{2,0,1:T(8,128)(2,1)} %bitcast.48), calls=%async_computation | async-start | bytes 1048576 | tf_op jit(solution)/shard_map/all_to_all | solution.py:100
  8.3 36.8 %copy-start.7 = (s32[1,512]{1,0:T(1,128)S(1)}, s32[1,512]{1,0:T(1,128)}, u32[]{:S(2)}) copy-start(s32[1,512]{1,0:T(1,128)} %param.15) | copy-start | bytes 6148
  8.3 36.8 %copy-start.6 = (s32[1,512]{1,0:T(1,128)S(1)}, s32[1,512]{1,0:T(1,128)}, u32[]{:S(2)}) copy-start(s32[1,512]{1,0:T(1,128)} %param.14) | copy-start | bytes 6148
  17.2 12.3 %all-to-all-start.1 = ((bf16[128,4,512]{2,0,1:T(8,128)(2,1)}), bf16[128,4,512]{2,0,1:T(8,128)(2,1)S(1)}, u32[]{:S(2)}, u32[]{:S(2)}) async-start(bf16[128,4,512]{2,0,1:T(8,128)(2,1)} %bitcast.47), calls=%async_computation.1 | async-start | bytes 1048576 | tf_op jit(solution)/shard_map/all_to_all | solution.py:101
  29.4 12.3 %all-to-all-start.2 = ((bf16[128,4,512]{2,0,1:T(8,128)(2,1)}), bf16[128,4,512]{2,0,1:T(8,128)(2,1)S(1)}, u32[]{:S(2)}, u32[]{:S(2)}) async-start(bf16[128,4,512]{2,0,1:T(8,128)(2,1)} %bitcast.46), calls=%async_computation.2 | async-start | bytes 1048576 | tf_op jit(solution)/shard_map/all_to_all | solution.py:102
  41.7 12.3 %all-to-all-start.4 = ((bf16[128,4,512]{2,0,1:T(8,128)(2,1)}), bf16[128,4,512]{2,0,1:T(8,128)(2,1)S(1)}, u32[]{:S(2)}, u32[]{:S(2)}) async-start(bf16[128,4,512]{2,0,1:T(8,128)(2,1)} %bitcast.45), calls=%async_computation.4 | async-start | bytes 1048576 | tf_op jit(solution)/shard_map/all_to_all | solution.py:106
  63.1 12.3 %all-to-all-start.7 = ((bf16[4,128,512]{2,1,0:T(8,128)(2,1)}), bf16[4,128,512]{2,1,0:T(8,128)(2,1)S(1)}, u32[]{:S(2)}, u32[]{:S(2)}) async-start(bf16[4,128,512]{2,1,0:T(8,128)(2,1)} %convert_element_type.117), calls=%async_computation.7 | async-start | bytes 1048576 | tf_op jit(solution)/shard_map/all_to_all | solution.py:113
  75.3 14.8 %all-to-all-start.3 = ((bf16[4,128,512]{2,1,0:T(8,128)(2,1)}), bf16[4,128,512]{2,1,0:T(8,128)(2,1)S(1)}, u32[]{:S(2)}, u32[]{:S(2)}) async-start(bf16[4,128,512]{2,1,0:T(8,128)(2,1)} %convert_element_type.99), calls=%async_computation.3 | async-start | bytes 1048576 | tf_op jit(solution)/shard_map/all_to_all | solution.py:105
  90.1 14.0 %all-to-all-start.6 = ((bf16[4,128,512]{1,2,0:T(8,128)(2,1)}), bf16[4,128,512]{1,2,0:T(8,128)(2,1)S(1)}, u32[]{:S(2)}, u32[]{:S(2)}) async-start(bf16[4,128,512]{1,2,0:T(8,128)(2,1)} %copy.81), calls=%async_computation.6 | async-start | bytes 1048576 | tf_op jit(solution)/shard_map/all_to_all | solution.py:112
  104.2 13.2 %all-to-all-start.5 = ((bf16[4,128,512]{1,2,0:T(8,128)(2,1)}), bf16[4,128,512]{1,2,0:T(8,128)(2,1)}, u32[]{:S(2)}, u32[]{:S(2)}) async-start(bf16[4,128,512]{1,2,0:T(8,128)(2,1)} %copy.77), calls=%async_computation.5 | async-start | bytes 1048576 | tf_op jit(solution)/shard_map/all_to_all | solution.py:111
  110.0 10.9 %copy-start = (bf16[128,2048]{1,0:T(8,128)(2,1)S(1)}, bf16[128,2048]{1,0:T(8,128)(2,1)}, u32[]{:S(2)}) copy-start(bf16[128,2048]{1,0:T(8,128)(2,1)} %param.8) | copy-start | bytes 1572868
  110.1 10.9 %copy-start.4 = (f32[2048]{0:T(1024)S(1)}, f32[2048]{0:T(1024)}, u32[]{:S(2)}) copy-start(f32[2048]{0:T(1024)} %param.11) | copy-start | bytes 24580
